TPU v7x, 128 devices: a whole 4x4x4 slice. The times are simulated.
128 devices in a mesh: row: 16 (over y, z), col: 8 (over x, core).
Axes of the slice: x: 4, y: 4, z: 4, core: 2. Of those that a mesh axis runs over, the one named last changes fastest.
Arguments:
- densities: bfloat16 [18432, 3072], P(('row', 'col')), may hold values from -0.796875 to 0.796875
- counts: int32 [2048], P(('row', 'col')), may hold values from 3 to 9
- coulomb: float32 [3072], replicated, may hold values from 0.05 to 1
- energies: float32 [18432], P(('row', 'col')), may hold values from 8 to 64
- vectors: bfloat16 [18432, 64], P(('row', 'col')), may hold values from -0.046875 to 0.046875
Outputs:
- kernel: float32 [18432, 18432], P('row', 'col')
- product: float32 [18432, 64], P(('row', 'col'))
All inputs are finite; a program needn't handle non-finite values.
Results may differ from a plain program's by a relative error of at most 0.0095.
Values may be sent and summed in bfloat16 or wider, within the bound.
A program may use at most 128 MiB of HBM per device.

v0:
```python
import jax
import jax.numpy as jnp
from jax import lax
from jax.sharding import Mesh
from jax.sharding import PartitionSpec as P

SLOT = 9
ROW = ("row_0", "row_1")
ROW_COL = ("row_0", "row_1", "col")


def gather_axes(value, axes, dim):
    filled = value
    for number in range(len(axes) - 1, -1, -1):
        filled = lax.all_gather(filled, axes[number], axis=dim, tiled=True)
    return filled


def split_up(value, dim, count):
    before, after = (value.shape[:dim], value.shape[dim + 1 :])
    return jnp.moveaxis(value.reshape(*before, count, -1, *after), dim, 0)


def sent_and_summed(value, axis, dim):
    count = lax.axis_size(axis)
    blocks = lax.all_to_all(split_up(value, dim, count), axis, 0, 0, tiled=True)
    return jnp.sum(blocks.astype(jnp.float32), axis=0)


def split_product(matrix, right_side):
    high = matrix.astype(jnp.bfloat16)
    rest = matrix - high.astype(jnp.float32)
    middle = rest.astype(jnp.bfloat16)
    lowest = (rest - middle.astype(jnp.float32)).astype(jnp.bfloat16)
    total = jnp.dot(high, right_side, preferred_element_type=jnp.float32)
    total = total + jnp.dot(middle, right_side, preferred_element_type=jnp.float32)
    return total + jnp.dot(lowest, right_side, preferred_element_type=jnp.float32)


def body(densities, counts, coulomb, energies, vectors):
    kpoints = counts.shape[0]
    slot_index = lax.broadcasted_iota(jnp.int32, (kpoints, SLOT), 1)
    usable = (slot_index < counts[:, None]).reshape(kpoints * SLOT)
    masked = jnp.where(usable[:, None], densities, jnp.zeros_like(densities))
    weighted = (masked.astype(jnp.float32) * coulomb[None, :]).astype(jnp.bfloat16)
    row_block = lax.all_gather(weighted, "col", axis=0, tiled=True)
    kernel = lax.dot_general(
        row_block,
        lax.all_gather(masked, ROW, axis=0, tiled=True),
        (((1,), (1,)), ((), ())),
        preferred_element_type=jnp.float32,
    )
    column_vectors = gather_axes(vectors, ROW, 0)
    partial_value = split_product(kernel, column_vectors)
    coupled = sent_and_summed(partial_value.astype(jnp.bfloat16), "col", 0)
    diagonal = jnp.where(usable, energies, jnp.zeros_like(energies))
    product = coupled + diagonal[:, None] * vectors.astype(jnp.float32)
    return (kernel, product)


def solution(mesh):
    finer = Mesh(mesh.devices.reshape(4, 4, mesh.shape["col"]), ("row_0", "row_1", "col"))
    in_specs = (P(ROW_COL, None), P(ROW_COL), P(), P(ROW_COL), P(ROW_COL, None))
    out_specs = (P(ROW, "col"), P(ROW_COL, None))
    return jax.shard_map(body, mesh=finer, in_specs=in_specs, out_specs=out_specs, check_vma=False)
```

profile of v0, /device:TPU:1, one launch (start us, length us, event | category | flops | bytes accessed | tf_op | source)
XLA Modules:
  0.0 206.2 jit_solution(9412224943959909971)
XLA Ops:
  7.2 0.0 all-gather.5.cloned.1.call-start
  7.2 0.7 iota_compare_fusion
  7.9 0.1 lt.18
  8.0 2.8 %multiply_convert_fusion = (bf16[144,3072]{1,0:T(8,128)(2,1)}, bf16[144,3072]{1,0:T(8,128)(2,1)}) fusion(f32[3072]{0:T(1024)} %param.7, bf16[144,3072]{1,0:T(8,128)(2,1)} %param.5, pred[144]{0:T(512)(128)(4,1)S(1)} %lt.18), kind=kLoop, calls=%fused_computation.10 | loop fusion | flops 1769472 | bytes 2666640 | tf_op jit(solution)/shard_map/convert_element_type | solution.py:45
  10.8 0.0 all-gather.5.cloned.1.call-update
  10.8 0.0 all-gather.7.cloned.1.call-start
  10.9 0.7 all-gather.7.cloned.1.call-update
  11.6 11.8 %all-gather = bf16[4,144,64]{1,2,0:T(8,128)(2,1)S(1)} all-gather(bf16[1,144,64]{1,2,0:T(8,128)(2,1)} %bitcast.12), channel_id=1, replica_groups=mesh['row_0'=4,'row_1'=4,'col'=8] {'row_1'}, dimensions={0}, use_global_device_ids=true | all-gather | bytes 92160 | tf_op jit(solution)/shard_map/all_gather | solution.py:15
  23.4 0.1 copy.10
  23.5 0.1 reshape.30
  23.6 11.2 %all-gather.1 = bf16[4,576,64]{1,2,0:T(8,128)(2,1)S(1)} all-gather(bf16[1,576,64]{1,2,0:T(8,128)(2,1)S(1)} %reshape.30), channel_id=1, replica_groups=mesh['row_0'=4,'row_1'=4,'col'=8] {'row_0'}, dimensions={0}, use_global_device_ids=true | all-gather | bytes 368640 | tf_op jit(solution)/shard_map/all_gather | solution.py:15
  34.9 0.3 copy.11
  35.1 0.3 reshape.31
  35.4 23.3 %all-gather.5.cloned.1.call-done = bf16[1152,3072]{1,0:T(8,128)(2,1)} async-done(((bf16[144,3072]{1,0:T(8,128)(2,1)}), bf16[1152,3072]{1,0:T(8,128)(2,1)}) %all-gather.5.cloned.1.call-update) | async-done | bytes 7077904 | tf_op jit(solution)/shard_map/all_gather | solution.py:46
  58.7 99.7 %all-gather.7.cloned.1.call-done = bf16[2304,3072]{1,0:T(8,128)(2,1)} async-done(((bf16[144,3072]{1,0:T(8,128)(2,1)}), bf16[2304,3072]{1,0:T(8,128)(2,1)}) %all-gather.7.cloned.1.call-update) | async-done | bytes 14155792 | tf_op jit(solution)/shard_map/all_gather | solution.py:49
  158.4 21.7 %fusion.11 = f32[1152,2304]{1,0:T(8,128)S(1)} fusion(bf16[1152,3072]{1,0:T(8,128)(2,1)} %all-gather.5.cloned.1.call-done, bf16[2304,3072]{1,0:T(8,128)(2,1)} %all-gather.7.cloned.1.call-done), kind=kOutput, calls=%fused_computation.16 | convolution fusion | flops 16307453952 | bytes 31850496 | tf_op jit(solution)/shard_map/dot_general | solution.py:47
  180.1 0.0 copy-start
  180.1 1.7 fusion.1
  181.9 1.8 fusion.7
  183.6 0.6 copy-done
  184.2 0.0 copy-start.2
  184.2 0.0 copy-start.1
  184.2 1.8 fusion.10
  186.0 0.4 reshape.27
  186.4 0.7 copy.12
  187.1 5.1 %all-to-all-start = ((bf16[8,144,64]{1,2,0:T(8,128)(2,1)}), bf16[8,144,64]{1,2,0:T(8,128)(2,1)S(1)}, u32[]{:S(2)}, u32[]{:S(2)}) async-start(bf16[8,144,64]{1,2,0:T(8,128)(2,1)} %copy.12), calls=%async_computation | async-start | bytes 524288 | tf_op jit(solution)/shard_map/all_to_all | solution.py:26
  192.2 0.0 copy-done.2
  192.2 6.5 %all-to-all-done = bf16[8,144,64]{1,2,0:T(8,128)(2,1)S(1)} async-done(((bf16[8,144,64]{1,2,0:T(8,128)(2,1)}), bf16[8,144,64]{1,2,0:T(8,128)(2,1)S(1)}, u32[]{:S(2)}, u32[]{:S(2)}) %all-to-all-start) | async-done | bytes 147488 | tf_op jit(solution)/shard_map/all_to_all | solution.py:26
  198.8 0.0 copy-done.1
  198.8 0.6 multiply_add_fusion
  (2 shorter events, 0.1 us)
Async XLA Ops:
  7.2 51.6 %all-gather.5.cloned.1.call-start = ((), (), s32[]{:S(2)}) async-start(), calls=%async_computation.1 | async-start | bytes 7962624 | tf_op jit(solution)/shard_map/all_gather | solution.py:46
  10.8 147.6 %all-gather.7.cloned.1.call-start = ((), (), s32[]{:S(2)}) async-start(), calls=%async_computation.2 | async-start | bytes 15040512 | tf_op jit(solution)/shard_map/all_gather | solution.py:49
  180.1 4.1 %copy-start = (f32[1152,2304]{1,0:T(8,128)}, f32[1152,2304]{1,0:T(8,128)S(1)}, u32[]{:S(2)}) copy-start(f32[1152,2304]{1,0:T(8,128)S(1)} %fusion.11) | copy-start | bytes 31850500
  184.2 8.0 %copy-start.2 = (f32[144]{0:T(256)S(1)}, f32[144]{0:T(256)}, u32[]{:S(2)}) copy-start(f32[144]{0:T(256)} %param.8) | copy-start | bytes 1732
  184.2 14.5 %copy-start.1 = (bf16[144,64]{0,1:T(8,128)(2,1)S(1)}, bf16[144,64]{0,1:T(8,128)(2,1)}, u32[]{:S(2)}) copy-start(bf16[144,64]{0,1:T(8,128)(2,1)} %param.9) | copy-start | bytes 55300
  187.1 11.6 %all-to-all-start = ((bf16[8,144,64]{1,2,0:T(8,128)(2,1)}), bf16[8,144,64]{1,2,0:T(8,128)(2,1)S(1)}, u32[]{:S(2)}, u32[]{:S(2)}) async-start(bf16[8,144,64]{1,2,0:T(8,128)(2,1)} %copy.12), calls=%async_computation | async-start | bytes 524288 | tf_op jit(solution)/shard_map/all_to_all | solution.py:26
Sparse Core Ops, SparseCore 0:
  11.0 47.7 all-gather.4
  60.9 97.4 all-gather.6
where the time goes:
time: 207 us; the launch traced here: 206 us
  waiting for transfers between devices  130 us (63%)
  matrix products  27 us (13%)
  blocking collectives  23 us (11%)
  between operations  14.1 us (7%)
  starting transfers between devices  5.17 us (2%)
  other arithmetic  4.2 us (2%)
  local copies, waits for them, and re-layouts  2.6 us (1%)
    all_gather x1, waiting for transfers between devices, body(): lax.all_gather(masked, ROW, axis=0, tiled=True)  99.7 us
    all_gather x1, waiting for transfers between devices, body(): row_block = lax.all_gather(weighted, 'col', axis=0, tiled=True)  23.3 us
    all_gather x2, blocking collectives, gather_axes(): filled = lax.all_gather(filled, axes[number], axis=dim, tiled=True)  23 us
    dot_general x1, matrix products, body(): lax.dot_general(row_block, lax.all_gather(masked, ROW, axis=0, tiled=True...  21.7 us
    all_to_all x1, waiting for transfers between devices, sent_and_summed(): blocks = lax.all_to_all(split_up(value, dim, count), axis, 0, 0, tiled=True)  6.46 us
    all_to_all x1, starting transfers between devices, sent_and_summed(): blocks = lax.all_to_all(split_up(value, dim, count), axis, 0, 0, tiled=True)  5.09 us
  transfers between devices with their start and end apart: 3, of which 3 were waited for; matrix products, arithmetic and copies ran while one was open for 0% of the time, Pallas kernels for 0%

commit v1 on v0

v1 whole, which is shorter than its diff:
```python
import functools

import jax
import jax.numpy as jnp
from jax import lax
from jax.experimental import pallas as pl
from jax.experimental.pallas import tpu as pltpu
from jax.sharding import PartitionSpec as P

MESH = pl.DeviceIdType.MESH
SLOT = 9
ROW_COL = ("row", "col")
NT = (((1,), (1,)), ((), ()))
DFS = (0, -1, 1, 2)
LAG2, LAG3, LAG4, LAGC = 1, 2, 3, 4
CHUNK = 256
COL_TILE = 768


def gather_kernel(
    dims,
    dens_ref,
    counts_ref,
    coul_ref,
    en_ref,
    vt_ref,
    acc,
    r_last,
    c_last,
    prod_ref,
    dn,
    wt,
    cbuf,
    rbuf,
    pb,
    rs1,
    qb,
    rs2,
    sb,
    rs3,
    tb,
    pf,
    in_sem,
    send_sem,
    recv_sem,
    psend,
    precv,
):
    blk, g_all, n_row, n_col = dims
    n = g_all // CHUNK
    nv = vt_ref.shape[0]
    half = CHUNK // 2
    row = lax.axis_index("row")
    col = lax.axis_index("col")
    core = col % 2
    first = (row // 4) * (1 - core) + (row % 4) * core
    second = (row % 4) * (1 - core) + (row // 4) * core

    def at(df, ds):
        f = (first + df + 4) % 4
        s = (second + ds + 4) % 4
        return f * (4 - 3 * core) + s * (1 + 3 * core)

    def xcol(dx, same=True):
        x = (col // 2 + dx + 4) % 4
        return 2 * x + (core if same else 1 - core)

    for g in range(n):
        lanes = slice(g * CHUNK, (g + 1) * CHUNK)
        pltpu.make_async_copy(dens_ref.at[:, lanes], dn.at[:, lanes], in_sem.at[g]).start()
    barrier = pltpu.get_barrier_semaphore()
    peers = [(row, (col + d) % n_col) for d in range(1, n_col)]
    peers += [(at(d, 0), col) for d in range(1, 4)] + [(at(0, d), col) for d in range(1, 4)]
    for peer in peers:
        pl.semaphore_signal(barrier, inc=1, device_id=peer, device_id_type=MESH)

    sub = lax.broadcasted_iota(jnp.int32, (blk, CHUNK), 0)
    lane = lax.broadcasted_iota(jnp.int32, (1, blk), 1)
    keep = sub < 0
    keep_lane = lane < 0
    for k in range(blk // SLOT):
        low, high = k * SLOT, k * SLOT + counts_ref[k]
        keep = keep | ((sub >= low) & (sub < high))
        keep_lane = keep_lane | ((lane >= low) & (lane < high))

    own_c = pl.multiple_of(row * blk, 16)
    own_r = pl.multiple_of(col * blk, 16)
    for g in range(n):
        lanes = slice(g * CHUNK, (g + 1) * CHUNK)
        pltpu.make_async_copy(dens_ref.at[:, lanes], dn.at[:, lanes], in_sem.at[g]).wait()
        masked = jnp.where(keep, dn[:, lanes].astype(jnp.float32), 0.0)
        weighted = (masked * coul_ref[:, lanes]).astype(jnp.bfloat16)
        masked = masked.astype(jnp.bfloat16)
        cbuf[g, pl.ds(own_c, blk), :] = masked
        rbuf[g, pl.ds(own_r, blk), :] = weighted
        dn[:, lanes] = masked
        wt[:, lanes] = weighted
    pl.semaphore_wait(barrier, len(peers))

    def copy(k, g, buf, block, part, peer):
        rows = pl.ds(pl.multiple_of(block * blk, 16), blk)
        lanes = {"all": pl.ds(0, CHUNK), "a": pl.ds(0, half), "b": pl.ds(half, half)}[part]
        ref = buf.at[g, rows, lanes]
        return pltpu.make_async_remote_copy(
            src_ref=ref,
            dst_ref=ref,
            send_sem=send_sem.at[g, k],
            recv_sem=recv_sem.at[g, k],
            device_id=peer,
            device_id_type=MESH,
        )

    fp, fm = (at(1, 0), col), (at(-1, 0), col)
    sp, sm = (at(0, 1), col), (at(0, -1), col)
    xp, xm = (row, xcol(1)), (row, xcol(-1))
    other = (row, xcol(0, False))
    kinds = [
        (cbuf, at(0, 0), "all", fp, at(-1, 0)),
        (cbuf, at(0, 0), "all", fm, at(1, 0)),
        (cbuf, at(-1, 0), "a", fp, at(2, 0)),
        (cbuf, at(1, 0), "b", fm, at(2, 0)),
    ]
    for df in DFS:
        kinds.append((cbuf, at(df, 0), "all", sp, at(df, -1)))
        kinds.append((cbuf, at(df, 0), "all", sm, at(df, 1)))
    for df in DFS:
        kinds.append((cbuf, at(df, -1), "a", sp, at(df, 2)))
        kinds.append((cbuf, at(df, 1), "b", sm, at(df, 2)))
    kinds += [
        (rbuf, xcol(0), "all", other, xcol(0, False)),
        (rbuf, xcol(0), "all", xp, xcol(-1)),
        (rbuf, xcol(0), "all", xm, xcol(1)),
        (rbuf, xcol(-1), "a", xp, xcol(2)),
        (rbuf, xcol(1), "b", xm, xcol(2)),
        (rbuf, xcol(-1), "all", other, xcol(-1, False)),
        (rbuf, xcol(1), "all", other, xcol(1, False)),
        (rbuf, xcol(2), "all", other, xcol(2, False)),
    ]

    def send(g, *ks):
        for k in ks:
            buf, block, part, peer, _ = kinds[k]
            copy(k, g, buf, block, part, peer).start()

    def got(g, *ks):
        for k in ks:
            buf, _, part, peer, block = kinds[k]
            copy(k, g, buf, block, part, peer).wait_recv()

    def stage1(g):
        send(g, 0, 1, 4, 5, 21, 22, 20)

    def stage2(g):
        got(g, 0)
        send(g, 2, 6, 7)
        got(g, 1)
        send(g, 3, 8, 9)
        got(g, 4)
        send(g, 12)
        got(g, 5)
        send(g, 13)
        got(g, 21)
        send(g, 23, 25)
        got(g, 22)
        send(g, 24, 26)

    def stage3(g):
        got(g, 2, 3)
        send(g, 10, 11)
        for k in (6, 7, 8, 9):
            got(g, k)
            send(g, k + 8)
        got(g, 23, 24)
        send(g, 27)

    def stage4(g):
        for k in (10, 11):
            got(g, k)
            send(g, k + 8)

    def arrived(g):
        got(g, 12, 13, 14, 15, 16, 17, 18, 19, 20, 25, 26, 27)

    def compute(g):
        @pl.loop(0, cbuf.shape[1] // COL_TILE)
        def _(j):
            lanes = pl.ds(pl.multiple_of(j * COL_TILE, COL_TILE), COL_TILE)
            acc[:, lanes] += lax.dot_general(
                rbuf[g], cbuf[g, lanes, :], NT, preferred_element_type=jnp.float32
            )

    width = g_all // n_col
    quarter = nv // 4

    def pcopy(k, src, dst, peer):
        return pltpu.make_async_remote_copy(
            src_ref=src,
            dst_ref=dst,
            send_sem=psend.at[k],
            recv_sem=precv.at[k],
            device_id=peer,
            device_id_type=MESH,
        )

    def to_cols(k0, src, dst, start):
        for d in range(1, n_col):
            to, frm = (col + d) % n_col, (col + n_col - d) % n_col
            slot = col if start else frm
            made = pcopy(k0 + d - 1, src(to), dst.at[slot], (row, to))
            if start:
                made.start()
            else:
                made.wait_recv()

    def ring_first(k0, src, dst, start):
        for d in range(1, 4):
            to = (first + d) % 4
            slot = first if start else (first + 4 - d) % 4
            made = pcopy(k0 + d - 1, src(to), dst.at[slot], (at(d, 0), col))
            if start:
                made.start()
            else:
                made.wait_recv()

    def ring_second(k0, src, dst, start):
        for d in range(1, 4):
            slot = second if start else (second + 4 - d) % 4
            made = pcopy(k0 + d - 1, src, dst.at[slot], (at(0, d), col))
            if start:
                made.start()
            else:
                made.wait_recv()

    def total(ref):
        value = ref[0].astype(jnp.float32)
        for i in range(1, ref.shape[0]):
            value = value + ref[i].astype(jnp.float32)
        return value

    def p_first():
        for i in range(n_col):
            part = jnp.dot(
                vt_ref[...], dn[:, i * width : (i + 1) * width], preferred_element_type=jnp.float32
            )
            pb[i] = part.astype(jnp.bfloat16)
        rs1[col] = pb[col]
        to_cols(0, lambda to: pb.at[to], rs1, True)

    def p_second():
        to_cols(0, lambda to: pb.at[to], rs1, False)
        value = total(rs1)
        for i in range(4):
            qb[i] = value[i * quarter : (i + 1) * quarter, :].astype(jnp.bfloat16)
        rs2[first] = qb[first]
        ring_first(7, lambda to: qb.at[to], rs2, True)

    def p_third():
        ring_first(7, lambda to: qb.at[to], rs2, False)
        value = total(rs2).astype(jnp.bfloat16)
        sb[...] = value
        rs3[second] = value
        ring_second(10, sb, rs3, True)

    def p_fourth():
        ring_second(10, sb, rs3, False)
        value = total(rs3).astype(jnp.bfloat16)
        sb2 = tb.at[first]
        sb2[...] = value
        ring_first(13, lambda to: tb.at[first], tb, True)

    def p_fifth():
        ring_first(13, lambda to: tb.at[first], tb, False)
        for i in range(4):
            pf[col, i * quarter : (i + 1) * quarter, :] = tb[i]
        to_cols(16, lambda to: pf.at[col], pf, True)

    def p_last():
        to_cols(16, lambda to: pf.at[col], pf, False)
        coupled = jnp.zeros((nv, blk), jnp.float32)
        for i in range(n_col):
            coupled = coupled + lax.dot_general(
                pf[i], wt[:, i * width : (i + 1) * width], NT, preferred_element_type=jnp.float32
            )
        diagonal = jnp.where(keep_lane, en_ref[...], 0.0)
        prod_ref[...] = coupled + diagonal * vt_ref[...].astype(jnp.float32)

    p_stages = (p_first, p_second, p_third, p_fourth, p_fifth, p_last)

    @pl.loop(0, n + LAG4)
    def _(t):
        def when(g, what):
            @pl.when((g >= 0) & (g < n))
            def _():
                what(g)

        when(t, stage1)
        when(t - LAG4, stage4)
        when(t - LAG3, stage3)
        when(t - LAG2, stage2)
        for i, stage in enumerate(p_stages):
            pl.when(t == i)(stage)

        @pl.when(t == 0)
        def _():
            @pl.loop(0, acc.shape[0] // 16)
            def _(i):
                rows = pl.ds(pl.multiple_of(i * 16, 16), 16)
                acc[rows, :] = jnp.zeros((16, acc.shape[1]), jnp.float32)

        @pl.when(t >= LAGC)
        def _():
            arrived(t - LAGC)
            compute(t - LAGC)

    for g in range(n + LAG4 - LAGC, n - 1):
        arrived(g)
        compute(g)
    arrived(n - 1)
    r_last[...] = rbuf[n - 1]
    c_last[...] = cbuf[n - 1]

    @pl.loop(0, n)
    def _(g):
        for k, (buf, block, part, peer, _) in enumerate(kinds):
            copy(k, g, buf, block, part, peer).wait_send()

    for d in range(1, n_col):
        to = (col + d) % n_col
        pcopy(d - 1, pb.at[to], rs1.at[col], (row, to)).wait_send()
        pcopy(15 + d, pf.at[col], pf.at[col], (row, to)).wait_send()
    for d in range(1, 4):
        to = (first + d) % 4
        pcopy(6 + d, qb.at[to], rs2.at[first], (at(d, 0), col)).wait_send()
        pcopy(9 + d, sb, rs3.at[second], (at(0, d), col)).wait_send()
        pcopy(12 + d, tb.at[first], tb.at[first], (at(d, 0), col)).wait_send()


def finish_kernel(acc, r_last, c_last, prod_in, out_ref, prod_out, stage, sem, psem):
    tile = stage.shape[2]
    steps = acc.shape[1] // tile
    product = pltpu.make_async_copy(prod_in, prod_out, psem)
    product.start()

    def out(j):
        return pltpu.make_async_copy(
            stage.at[j], out_ref.at[:, j * tile : (j + 1) * tile], sem.at[j]
        )

    for j in range(steps):
        lanes = slice(j * tile, (j + 1) * tile)
        stage[j] = acc[:, lanes] + lax.dot_general(
            r_last[...], c_last[lanes, :], NT, preferred_element_type=jnp.float32
        )
        out(j).start()
    for j in range(steps):
        out(j).wait()
    product.wait()


def solution(mesh):
    n_row, n_col = mesh.shape["row"], mesh.shape["col"]

    def body(densities, counts, coulomb, energies, vectors):
        blk, g_all = densities.shape
        nv = vectors.shape[1]
        n = g_all // CHUNK
        bf, f32 = jnp.bfloat16, jnp.float32
        rows, cols = n_col * blk, n_row * blk
        width = g_all // n_col
        dma = pltpu.SemaphoreType.DMA
        vmem = pl.BlockSpec(memory_space=pltpu.VMEM)
        acc, r_last, c_last, prod = pl.pallas_call(
            functools.partial(gather_kernel, (blk, g_all, n_row, n_col)),
            out_shape=(
                pltpu.VMEM((rows, cols), f32),
                pltpu.VMEM((rows, CHUNK), bf),
                pltpu.VMEM((cols, CHUNK), bf),
                pltpu.VMEM((nv, blk), f32),
            ),
            in_specs=[
                pl.BlockSpec(memory_space=pl.ANY),
                pl.BlockSpec(memory_space=pltpu.SMEM),
                vmem,
                vmem,
                vmem,
            ],
            out_specs=(vmem,) * 4,
            scratch_shapes=[
                pltpu.VMEM((blk, g_all), bf),
                pltpu.VMEM((blk, g_all), bf),
                pltpu.VMEM((n, cols, CHUNK), bf),
                pltpu.VMEM((n, rows, CHUNK), bf),
                pltpu.VMEM((n_col, nv, width), bf),
                pltpu.VMEM((n_col, nv, width), bf),
                pltpu.VMEM((4, nv // 4, width), bf),
                pltpu.VMEM((4, nv // 4, width), bf),
                pltpu.VMEM((nv // 4, width), bf),
                pltpu.VMEM((4, nv // 4, width), bf),
                pltpu.VMEM((4, nv // 4, width), bf),
                pltpu.VMEM((n_col, nv, width), bf),
                dma((n,)),
                dma((n, 28)),
                dma((n, 28)),
                dma((23,)),
                dma((23,)),
            ],
            compiler_params=pltpu.CompilerParams(
                collective_id=0, has_side_effects=True, vmem_limit_bytes=40 * 2**20
            ),
            name="gather",
        )(densities, counts, coulomb[None, :], energies[None, :], vectors.T)
        kernel, product = pl.pallas_call(
            finish_kernel,
            out_shape=(
                jax.ShapeDtypeStruct((rows, cols), f32),
                jax.ShapeDtypeStruct((nv, blk), f32),
            ),
            in_specs=[vmem] * 4,
            out_specs=(pl.BlockSpec(memory_space=pl.ANY),) * 2,
            scratch_shapes=[
                pltpu.VMEM((cols // CHUNK, rows, CHUNK), f32),
                dma((cols // CHUNK,)),
                dma,
            ],
            compiler_params=pltpu.CompilerParams(vmem_limit_bytes=40 * 2**20),
            name="finish",
        )(acc, r_last, c_last, prod)
        return kernel, product.T

    specs = (P(ROW_COL, None), P(ROW_COL), P(), P(ROW_COL), P(ROW_COL, None))
    return jax.shard_map(
        body,
        mesh=mesh,
        in_specs=specs,
        out_specs=(P("row", "col"), P(ROW_COL, None)),
        check_vma=False,
    )
```

time: 207 us -> 107 us (0.52)
  waiting for transfers between devices: 130 us -> 0 us
  Pallas kernels: 0 us -> 102 us
  matrix products: 27 us -> 0 us
  blocking collectives: 23 us -> 0 us
  between operations: 14.1 us -> 0.65 us
  starting transfers between devices: 5.17 us -> 0 us
  other arithmetic: 4.2 us -> 0 us
    all_gather x2 -> x0, waiting for transfers between devices: 123 us -> none  [the longest x1 99.7 us: body(): lax.all_gather(masked, ROW, axis=0, tiled=True)]
    pallas_call x0 -> x2, Pallas kernels: none -> 102 us  [the longest x1 97.4 us: body(): pl.pallas_call(functools.partial(gather_kernel, (blk, g_all, n_row, n_col...]
    dot_general x4 -> x0, matrix products: 27 us -> none  [the longest x1 21.7 us: body(): lax.dot_general(row_block, lax.all_gather(masked, ROW, axis=0, tiled=True...]
    all_gather x2 -> x0, blocking collectives: 23 us -> none  [gather_axes(): filled = lax.all_gather(filled, axes[number], axis=dim, tiled=True)]
    all_to_all x1 -> x0, waiting for transfers between devices: 6.46 us -> none  [sent_and_summed(): blocks = lax.all_to_all(split_up(value, dim, count), axis, 0, 0, tiled=True)]
    all_to_all x1 -> x0, starting transfers between devices: 5.09 us -> none  [sent_and_summed(): blocks = lax.all_to_all(split_up(value, dim, count), axis, 0, 0, tiled=True)]
    unnamed x8 -> x10, local copies, waits for them, and re-layouts: 1.04 us -> 3.96 us
    convert_element_type x1 -> x0, other arithmetic: 2.78 us -> none  [body(): (masked.astype(jnp.float32) * coulomb[None, :]).astype(jnp.bfloat16)]
  transfers between devices with their start and end apart: 3 -> 0, of which waited for: 3 -> 0; matrix products, arithmetic and copies ran while one was open for 0% -> 0% of each run, Pallas kernels for 0% -> 0%
where the time goes in v1:
time: 107 us; the launch traced here: 106 us
  Pallas kernels  102 us (95%)
  local copies, waits for them, and re-layouts  3.96 us (4%)
    pallas_call x1, Pallas kernels, body(): pl.pallas_call(functools.partial(gather_kernel, (blk, g_all, n_row, n_col...  97.4 us
    pallas_call x1, Pallas kernels, body(): pl.pallas_call(finish_kernel, out_shape=(jax.ShapeDtypeStruct((rows, cols...  4.48 us
    unnamed x10, local copies, waits for them, and re-layouts  3.96 us

profile of v1, /device:TPU:1, one launch (start us, length us, event | category | flops | bytes accessed | tf_op | source)
XLA Modules:
  0.0 106.5 jit_solution(5337365490192710350)
XLA Ops:
  0.6 0.0 copy-start
  0.6 1.2 %copy-done = bf16[144,3072]{1,0:T(8,128)(2,1)S(1)} copy-done((bf16[144,3072]{1,0:T(8,128)(2,1)S(1)}, bf16[144,3072]{1,0:T(8,128)(2,1)}, u32[]{:S(2)}) %copy-start) | copy-done | bytes 884760
  1.8 0.0 copy-start.1
  1.8 0.8 copy-done.1
  2.6 0.0 copy-start.2
  2.6 0.7 copy-done.2
  3.3 0.0 copy-start.3
  3.3 0.7 copy-done.3
  3.9 0.0 copy-start.4
  3.9 0.7 copy-done.4
  4.6 97.4 %gather.1 = (f32[1152,2304]{1,0:T(8,128)S(1)}, bf16[1152,256]{1,0:T(8,128)(2,1)S(1)}, bf16[2304,256]{1,0:T(8,128)(2,1)S(1)}, f32[64,144]{1,0:T(8,128)S(1)}) custom-call(bf16[144,3072]{1,0:T(8,128)(2,1)S(1)} %copy-done, s32[16]{0:T(128)S(1)} %copy-done.4, f32[1,3072]{1,0:T(1,128)S(1)} %bitcast.5, f32[1,144]{1,0:T(1,128)S(1)} %bitcast.6, ...), custom_call_target="tpu_custom_call" | custom-call | tf_op jit(solution)/shard_map/gather/pallas_call | solution.py:372
  102.0 4.5 %finish.1 = (f32[1152,2304]{1,0:T(8,128)}, f32[64,144]{1,0:T(8,128)}) custom-call(f32[1152,2304]{1,0:T(8,128)S(1)} %get-tuple-element.8.acc, bf16[1152,256]{1,0:T(8,128)(2,1)S(1)} %get-tuple-element.9.r_last, bf16[2304,256]{1,0:T(8,128)(2,1)S(1)} %get-tuple-element.10.c_last, f32[64,144]{1,0:T(8,128)S(1)} %get-tuple-element.11.prod_in), custom_call_target="tpu_custom_call" | custom-call | tf_op jit(solution)/shard_map/finish/pallas_call | solution.py:412
Async XLA Ops:
  0.6 1.2 %copy-start = (bf16[144,3072]{1,0:T(8,128)(2,1)S(1)}, bf16[144,3072]{1,0:T(8,128)(2,1)}, u32[]{:S(2)}) copy-start(bf16[144,3072]{1,0:T(8,128)(2,1)} %dens_ref.1) | copy-start | bytes 2654212
  1.8 0.8 copy-start.1
  2.6 0.7 copy-start.2
  3.3 0.7 copy-start.3
  3.9 0.7 copy-start.4
